TPU v7x, 32 devices: a whole 2x2x4 slice. The times are simulated.
32 devices in a mesh: cuts: 16 (over z, y, x), site: 2 (over core).
Axes of the slice: x: 2, y: 2, z: 4, core: 2. Of those that a mesh axis runs over, the one named last changes fastest.
Arguments:
- field: float32 [16, 2048], P('cuts'), may hold values from -4 to 4
- momenta: float32 [16, 2048], P('cuts'), may hold values from -4 to 4
- start_force: float32 [16, 2048], P('cuts'), may hold values from -4 to 4
- green: bfloat16 [16, 2048, 2048], P('cuts', 'site'), as said below
- forward_prop: bfloat16 [2048, 2048], P('site')
- back_prop: bfloat16 [2048, 2048], P('site')
- accept: int32 [16], P('cuts'), may hold values from 0 to 1
Outputs:
- new_field: float32 [16, 2048], P('cuts')
- new_momenta: float32 [16, 2048], P('cuts')
- new_force: float32 [16, 2048], P('cuts')
- energy_change: float32 [1], replicated
Inputs may be any that keep to these rules, and one draw needn't show every extreme that they name: green has a diagonal of 0.2 to 0.8 plus full-rank off-diagonal entries; the propagators are the identity plus full-rank entries.
All inputs are finite; a program needn't handle non-finite values.
Results may differ from a plain program's by a relative error of at most 0.0029.
Values may be sent and summed in bfloat16 or wider, within the bound.
A program may use at most 128 MiB of HBM per device.

v0:
```python
import jax
import jax.numpy as jnp
from jax import lax
from jax.sharding import PartitionSpec as P

coupling = 0.5
stepsize = 0.2


def from_behind(shard, axis, by):
    size = lax.axis_size(axis)
    return lax.ppermute(shard, axis, [(i, (i + by) % size) for i in range(size)])


def on_device(field, momenta, start_force, green, forward_prop, back_prop, accept):
    half = momenta - 0.5 * stepsize * start_force
    trial = field + stepsize * half
    start_local = jnp.sum(momenta * momenta) + jnp.sum(field * field)
    start_total = lax.psum(start_local, "cuts")
    source = green[0]
    phase = from_behind(trial[0], "cuts", -1)
    rows = source.shape[0]
    row_start = lax.axis_index("site") * rows
    growth = jnp.exp(coupling * phase)
    row_growth = lax.dynamic_slice_in_dim(growth, row_start, rows)
    scaled = (row_growth[:, None] * source.astype(jnp.float32)).astype(jnp.bfloat16)
    wrapped = jnp.dot(
        forward_prop,
        lax.all_gather(scaled, "site", axis=0, tiled=True),
        preferred_element_type=jnp.float32,
    )
    shrink = jnp.exp(-coupling * phase)
    diag_part = jnp.sum(wrapped * (shrink[None, :] * back_prop.astype(jnp.float32)), axis=1)
    diag_part = from_behind(diag_part, "cuts", 1)
    diagonal = lax.all_gather(diag_part, "site", axis=0, tiled=True)
    new_force = trial - 2.0 * coupling * (1.0 - 2.0 * diagonal[None, :])
    new_momenta = half - 0.5 * stepsize * new_force
    end_local = jnp.sum(new_momenta * new_momenta) + jnp.sum(trial * trial)
    total = lax.psum(end_local, "cuts") - start_total
    count = lax.axis_size("cuts") * field.shape[0] * field.shape[1]
    change = total / (2.0 * jnp.sqrt(jnp.float32(count)))
    new_field = jnp.where(accept[0] == 1, trial, field)
    return (new_field, new_momenta, new_force, jnp.reshape(change, (1,)))


def solution(mesh):
    return jax.shard_map(
        on_device,
        mesh=mesh,
        in_specs=(
            P("cuts", None),
            P("cuts", None),
            P("cuts", None),
            P("cuts", "site", None),
            P("site", None),
            P("site", None),
            P("cuts"),
        ),
        out_specs=(P("cuts", None), P("cuts", None), P("cuts", None), P()),
        check_vma=False,
    )
```

profile of v0, /device:TPU:0, one launch (start us, length us, event | category | flops | bytes accessed | tf_op | source)
XLA Modules:
  0.0 117.4 jit_solution(9493976677121686832)
XLA Ops:
  7.2 0.0 all-gather.2.cloned.1.call-start
  7.2 1.4 %multiply_reduce_fusion.2 = (f32[]{:T(128)}, f32[1,2048]{1,0:T(1,128)S(1)}, f32[]{:T(128)}, f32[]{:T(128)}) fusion(f32[1,2048]{1,0:T(1,128)} %param.7, f32[1,2048]{1,0:T(1,128)} %param.8, f32[1,2048]{1,0:T(1,128)} %param.9), kind=kLoop, calls=%fused_computation.7 | loop fusion | flops 20477 | bytes 32780 | tf_op jit(solution)/shard_map/reduce_sum | solution.py:38
  8.6 7.0 %collective-permute-start = (f32[2048]{0:T(1024)S(1)}, f32[2048]{0:T(1024)S(1)}, u32[]{:S(2)}, u32[]{:S(2)}) collective-permute-start(f32[2048]{0:T(1024)S(1)} %bitcast.14), channel_id=1, source_target_pairs={{0,30},{2,0},{4,2},{6,4},{8,6},{10,8},{12,10},{14,12},{16,14},{18,... | collective-permute-start | bytes 24584 | tf_op jit(solution)/shard_map/ppermute | solution.py:12
  15.5 1.4 %collective-permute-done = f32[2048]{0:T(1024)S(1)} collective-permute-done((f32[2048]{0:T(1024)S(1)}, f32[2048]{0:T(1024)S(1)}, u32[]{:S(2)}, u32[]{:S(2)}) %collective-permute-start) | collective-permute-done | bytes 8224 | tf_op jit(solution)/shard_map/ppermute | solution.py:12
  16.9 4.9 %fusion = bf16[1024,2048]{1,0:T(8,128)(2,1)} fusion(bf16[1,1024,2048]{2,1,0:T(8,128)(2,1)} %param.10, f32[1024]{0:T(1024)S(1)} %fusion.2), kind=kLoop, calls=%fused_computation.1 | loop fusion | flops 6291456 | bytes 8392704 | tf_op jit(solution)/shard_map/convert_element_type | solution.py:26
  21.8 0.0 all-gather.2.cloned.1.call-update
  21.8 6.4 %copy.12 = bf16[1024,2048]{0,1:T(8,128)(2,1)} copy(bf16[1024,2048]{1,0:T(8,128)(2,1)} %param.12) | data formatting | bytes 8388608 | tf_op args[5]
  28.2 0.0 copy-start
  28.3 0.0 copy-start.1
  28.3 0.0 copy-start.2
  28.3 15.2 %all-gather.2.cloned.1.call-done = bf16[2048,2048]{1,0:T(8,128)(2,1)} async-done(((bf16[1024,2048]{1,0:T(8,128)(2,1)}), bf16[2048,2048]{1,0:T(8,128)(2,1)}) %all-gather.2.cloned.1.call-update) | async-done | bytes 8388624 | tf_op jit(solution)/shard_map/all_gather | solution.py:29
  43.5 14.1 %fusion.1 = f32[1024]{0:T(1024)S(1)} fusion(bf16[1024,2048]{0,1:T(8,128)(2,1)} %copy.12, f32[2048]{0:T(1024)S(1)} %multiply_exponential_fusion, bf16[2048,2048]{1,0:T(8,128)(2,1)} %all-gather.2.cloned.1.call-done, bf16[1024,2048]{1,0:T(8,128)(2,1)} %param.11), kind=kOutput, calls=%fused_computation.3 | convolution fusion | flops 8598322176 | bytes 16789504 | tf_op jit(solution)/shard_map/dot_general | solution.py:27
  57.6 1.8 %collective-permute-start.1 = (f32[1024]{0:T(1024)S(1)}, f32[1024]{0:T(1024)S(1)}, u32[]{:S(2)}, u32[]{:S(2)}) collective-permute-start(f32[1024]{0:T(1024)S(1)} %fusion.1), channel_id=1, source_target_pairs={{0,2},{2,4},{4,6},{6,8},{8,10},{10,12},{12,14},{14,16},{16,18},{18... | collective-permute-start | bytes 12296 | tf_op jit(solution)/shard_map/ppermute | solution.py:12
  61.3 3.5 %collective-permute-done.1 = f32[1024]{0:T(1024)S(1)} collective-permute-done((f32[1024]{0:T(1024)S(1)}, f32[1024]{0:T(1024)S(1)}, u32[]{:S(2)}, u32[]{:S(2)}) %collective-permute-start.1) | collective-permute-done | bytes 4128 | tf_op jit(solution)/shard_map/ppermute | solution.py:12
  64.8 1.8 %all_gather.7 = f32[2048]{0:T(1024)S(1)} all-gather(f32[1024]{0:T(1024)S(1)} %collective-permute-done.1), channel_id=1, replica_groups=mesh['cuts'=16,'site'=2] {'site'}, dimensions={0}, use_global_device_ids=true | all-gather | bytes 12288 | tf_op jit(solution)/shard_map/all_gather | solution.py:35
  66.6 0.0 copy-done
  66.7 0.0 copy-done.1
  66.7 0.0 copy-done.2
  66.7 1.2 %multiply_reduce_fusion.3 = (f32[]{:T(128)}, f32[1,2048]{1,0:T(1,128)}, f32[1,2048]{1,0:T(1,128)}, f32[1,2048]{1,0:T(1,128)}) fusion(f32[1,2048]{1,0:T(1,128)S(1)} %copy-done, f32[1,2048]{1,0:T(1,128)S(1)} %copy-done.1, f32[1,2048]{1,0:T(1,128)S(1)} %get-tuple-element.7, f32[1,2048]{1,0:T(1,128)S(1)} %bitcast.13, f32[1,2048]{1,0:T(1,128)S(1)} %copy-done.2, ...), kind=kLoop, calls=%fused_computation.8 | loop fusion | flops 16383 | bytes 65541 | tf_op jit(solution)/shard_map/reduce_sum | solution.py:38
  69.1 39.0 %all-reduce = (f32[]{:T(128)}, f32[]{:T(128)}) all-reduce(f32[]{:T(128)S(6)} %add.18, f32[]{:T(128)S(6)} %add.19), channel_id=1, replica_groups=mesh['cuts'=16,'site'=2] {'cuts'}, use_global_device_ids=true, to_apply=%region_3.0 | all-reduce | flops 2 | bytes 16 | tf_op jit(solution)/shard_map/psum | solution.py:39
  (3 shorter events, 0.0 us)
Async XLA Ops:
  7.2 36.3 %all-gather.2.cloned.1.call-start = ((), (), s32[]{:S(2)}) async-start(), calls=%async_computation | async-start | bytes 12582912 | tf_op jit(solution)/shard_map/all_gather | solution.py:29
  8.6 8.3 %collective-permute-start = (f32[2048]{0:T(1024)S(1)}, f32[2048]{0:T(1024)S(1)}, u32[]{:S(2)}, u32[]{:S(2)}) collective-permute-start(f32[2048]{0:T(1024)S(1)} %bitcast.14), channel_id=1, source_target_pairs={{0,30},{2,0},{4,2},{6,4},{8,6},{10,8},{12,10},{14,12},{16,14},{18,... | collective-permute-start | bytes 24584 | tf_op jit(solution)/shard_map/ppermute | solution.py:12
  28.2 38.4 %copy-start = (f32[1,2048]{1,0:T(1,128)S(1)}, f32[1,2048]{1,0:T(1,128)}, u32[]{:S(2)}) copy-start(f32[1,2048]{1,0:T(1,128)} %param.8) | copy-start | bytes 24580
  28.3 38.4 %copy-start.1 = (f32[1,2048]{1,0:T(1,128)S(1)}, f32[1,2048]{1,0:T(1,128)}, u32[]{:S(2)}) copy-start(f32[1,2048]{1,0:T(1,128)} %param.9) | copy-start | bytes 24580
  28.3 38.4 %copy-start.2 = (f32[1,2048]{1,0:T(1,128)S(1)}, f32[1,2048]{1,0:T(1,128)}, u32[]{:S(2)}) copy-start(f32[1,2048]{1,0:T(1,128)} %param.7) | copy-start | bytes 24580
  57.6 7.3 %collective-permute-start.1 = (f32[1024]{0:T(1024)S(1)}, f32[1024]{0:T(1024)S(1)}, u32[]{:S(2)}, u32[]{:S(2)}) collective-permute-start(f32[1024]{0:T(1024)S(1)} %fusion.1), channel_id=1, source_target_pairs={{0,2},{2,4},{4,6},{6,8},{8,10},{10,12},{12,14},{14,16},{16,18},{18... | collective-permute-start | bytes 12296 | tf_op jit(solution)/shard_map/ppermute | solution.py:12
Sparse Core Ops, SparseCore 0:
  22.0 21.4 all-gather.1
where the time goes:
time: 118 us; the launch traced here: 117 us
  blocking collectives  40.8 us (35%)
  waiting for transfers between devices  20.1 us (17%)
  between operations  19.7 us (17%)
  matrix products  14.1 us (12%)
  starting transfers between devices  8.79 us (7%)
  other arithmetic  7.51 us (6%)
  local copies, waits for them, and re-layouts  6.42 us (5%)
    psum x1, blocking collectives, on_device(): total = lax.psum(end_local, 'cuts') - start_total  39 us
    all_gather x1, waiting for transfers between devices, on_device(): lax.all_gather(scaled, 'site', axis=0, tiled=True)  15.2 us
    dot_general x1, matrix products, on_device(): jnp.dot(forward_prop, lax.all_gather(scaled, 'site', axis=0, tiled=True),...  14.1 us
    ppermute x2, starting transfers between devices, from_behind(): lax.ppermute(shard, axis, [(i, (i + by) % size) for i in range(size)])  8.75 us
    unnamed x7, local copies, waits for them, and re-layouts  6.42 us
    convert_element_type x1, other arithmetic, on_device(): (row_growth[:, None] * source.astype(jnp.float32)).astype(jnp.bfloat16)  4.89 us
    ppermute x2, waiting for transfers between devices, from_behind(): lax.ppermute(shard, axis, [(i, (i + by) % size) for i in range(size)])  4.89 us
    reduce_sum x2, other arithmetic, on_device(): end_local = jnp.sum(new_momenta * new_momenta) + jnp.sum(trial * trial)  2.6 us
  transfers between devices with their start and end apart: 3, of which 3 were waited for; matrix products, arithmetic and copies ran while one was open for 5% of the time, Pallas kernels for 0%

commit v1 on v0

v1 whole, which is shorter than its diff:
```python
import functools

import jax
import jax.numpy as jnp
from jax import lax
from jax.experimental import pallas as pl
from jax.experimental.pallas import tpu as pltpu
from jax.sharding import PartitionSpec as P

coupling = 0.5
stepsize = 0.2
LANES = 128
WIDTH = 256
F32 = jnp.float32
MESH = pl.DeviceIdType.MESH


def group_of(slices):
    return max(d for d in range(1, slices + 1) if slices % d == 0 and d * d <= slices)


def half_of(momenta, force):
    return momenta - 0.5 * stepsize * force


def kernel(
    slices, sites, group, count,
    field, momenta, force, green, forward, back, accept,
    new_field, new_momenta, new_force, change,
    own, ahead, mine, other, fwd, bck, grow, shrink, acc, part, diag_out, diag_in, near, far,
    row_sem, load_sem, row_send, row_recv, green_send, green_recv,
    diag_send, diag_recv, near_send, near_recv, far_send, far_recv,
):
    cut = lax.axis_index("cuts")
    site = lax.axis_index("site")
    rows = mine.shape[0]
    size = own.shape[2]
    chunks = green_send.shape[0]
    deep = rows // chunks
    groups = slices // group
    behind = lax.rem(cut + slices - 1, slices)
    after = lax.rem(cut + 1, slices)
    base = (cut // group) * group
    spot = lax.rem(cut, group)
    block = cut // group
    slot = spot * sites + site

    near_peers = []
    for step in range(1, group * sites):
        peer = lax.rem(slot + step, group * sites)
        near_peers.append((peer, {"cuts": base + peer // sites, "site": lax.rem(peer, sites)}))
    far_peers = []
    for step in range(1, groups):
        peer = lax.rem(block + step, groups)
        far_peers.append((peer, {"cuts": peer * group + spot, "site": site}))
    partner = {"cuts": cut, "site": 1 - site}

    barrier = pltpu.get_barrier_semaphore()
    greet = [p for _, p in near_peers] + [p for _, p in far_peers]
    greet += [{"cuts": c, "site": s} for c in (behind, after) for s in range(sites)]
    for p in greet:
        pl.semaphore_signal(barrier, inc=1, device_id=p, device_id_type=MESH)

    row_loads = [
        pltpu.make_async_copy(src, own.at[i], row_sem.at[i])
        for i, src in enumerate((field, momenta, force))
    ]
    for c in row_loads:
        c.start()
    green_loads = [
        pltpu.make_async_copy(
            green.at[0, pl.ds(i * deep, deep)], mine.at[pl.ds(i * deep, deep)], load_sem.at[i]
        )
        for i in range(chunks)
    ]
    for c in green_loads:
        c.start()
    fwd_loads = [
        pltpu.make_async_copy(
            forward.at[:, pl.ds(pl.multiple_of(k * rows, LANES), rows)],
            fwd.at[i],
            load_sem.at[chunks + i],
        )
        for i, k in enumerate((site, 1 - site))
    ]
    back_load = pltpu.make_async_copy(back, bck, load_sem.at[chunks + 2])
    fwd_loads[0].start()
    back_load.start()
    fwd_loads[1].start()

    for c in row_loads:
        c.wait()
    pl.semaphore_wait(barrier, len(greet))

    row_sends = [
        pltpu.make_async_remote_copy(
            own.at[i], ahead.at[i], row_send.at[i], row_recv.at[i],
            device_id={"cuts": behind, "site": site}, device_id_type=MESH,
        )
        for i in range(3)
    ]
    for c in row_sends:
        c.start()
    green_sends = [
        pltpu.make_async_remote_copy(
            mine.at[pl.ds(i * deep, deep)], other.at[pl.ds(i * deep, deep)],
            green_send.at[i], green_recv.at[i],
            device_id=partner, device_id_type=MESH,
        )
        for i in range(chunks)
    ]
    for load, send in zip(green_loads, green_sends):
        load.wait()
        send.start()

    half = half_of(own[1], own[2])
    trial = own[0] + stepsize * half
    new_field[...] = jnp.where(accept[0] == 1, trial, own[0])

    for c in row_sends:
        c.wait_recv()
    phase = ahead[0] + stepsize * half_of(ahead[1], ahead[2])
    shrink[...] = jnp.exp(-coupling * phase)
    ahead_rows = pl.ds(pl.multiple_of(site * rows, LANES), rows)
    other_rows = pl.ds(pl.multiple_of((1 - site) * rows, LANES), rows)
    for h, where in enumerate((ahead_rows, other_rows)):
        line = ahead[0, :, where] + stepsize * half_of(ahead[1, :, where], ahead[2, :, where])
        line = jnp.exp(coupling * line)
        for b in range(rows // LANES):
            tile = jnp.broadcast_to(line[:, b * LANES:(b + 1) * LANES], (LANES, LANES))
            grow[h, b * LANES:(b + 1) * LANES, :] = tile.T
    part[...] = jnp.zeros_like(part)

    def product(h, source, columns):
        g = source[:, columns].astype(F32)
        e = grow[h]
        scaled = jnp.concatenate(
            [
                (e * g[:, i:i + LANES]).astype(jnp.bfloat16)
                for i in range(0, WIDTH, LANES)
            ],
            axis=1,
        )
        return jnp.dot(fwd[h], scaled, preferred_element_type=F32)

    fwd_loads[0].wait()

    @pl.loop(0, size // WIDTH)
    def _(j):
        columns = pl.ds(pl.multiple_of(j * WIDTH, WIDTH), WIDTH)
        acc[:, columns] = product(0, mine, columns)

    back_load.wait()
    fwd_loads[1].wait()
    for c in green_sends:
        c.wait_recv()

    @pl.loop(0, size // WIDTH)
    def _(j):
        columns = pl.ds(pl.multiple_of(j * WIDTH, WIDTH), WIDTH)
        wrapped = acc[:, columns] + product(1, other, columns)
        terms = wrapped * (shrink[:, columns] * bck[:, columns].astype(F32))
        total = part[...]
        for i in range(0, WIDTH, LANES):
            total = total + terms[:, i:i + LANES]
        part[...] = total

    line = jnp.concatenate(
        [
            jnp.sum(part[b * LANES:(b + 1) * LANES, :].T, axis=0, keepdims=True)
            for b in range(rows // LANES)
        ],
        axis=1,
    )
    diag_out[...] = line
    diag_sends = [
        pltpu.make_async_remote_copy(
            diag_out, diag_in.at[site], diag_send.at[s], diag_recv.at[site],
            device_id={"cuts": after, "site": s}, device_id_type=MESH,
        )
        for s in range(sites)
    ]
    for c in diag_sends:
        c.start()

    f, m = ahead[0, :, ahead_rows], ahead[1, :, ahead_rows]
    h = half_of(m, ahead[2, :, ahead_rows])
    t = f + stepsize * h
    n = h - 0.5 * stepsize * (t - 2.0 * coupling * (1.0 - 2.0 * line))
    energy = (n * n - m * m) + (t * t - f * f)
    lump = energy[:, :LANES]
    for i in range(LANES, rows, LANES):
        lump = lump + energy[:, i:i + LANES]
    near[slot] = lump
    near_sends = [
        pltpu.make_async_remote_copy(
            near.at[slot], near.at[slot], near_send.at[i], near_recv.at[slot],
            device_id=p, device_id_type=MESH,
        )
        for i, (_, p) in enumerate(near_peers)
    ]
    for c in near_sends:
        c.start()
    for peer, _ in near_peers:
        pltpu.make_async_copy(near.at[peer], near.at[peer], near_recv.at[peer]).wait()
    lump = near[0]
    for i in range(1, group * sites):
        lump = lump + near[i]
    far[block] = lump
    far_sends = [
        pltpu.make_async_remote_copy(
            far.at[block], far.at[block], far_send.at[i], far_recv.at[block],
            device_id=p, device_id_type=MESH,
        )
        for i, (_, p) in enumerate(far_peers)
    ]
    for c in far_sends:
        c.start()

    for s in range(sites):
        pltpu.make_async_copy(diag_in.at[s], diag_in.at[s], diag_recv.at[s]).wait()
    diagonal = jnp.concatenate([diag_in[s] for s in range(sites)], axis=1)
    force_now = trial - 2.0 * coupling * (1.0 - 2.0 * diagonal)
    new_force[...] = force_now
    new_momenta[...] = half - 0.5 * stepsize * force_now

    for peer, _ in far_peers:
        pltpu.make_async_copy(far.at[peer], far.at[peer], far_recv.at[peer]).wait()
    lump = far[0]
    for i in range(1, groups):
        lump = lump + far[i]
    change[0] = jnp.sum(lump) * (1.0 / (2.0 * count ** 0.5))

    for c in row_sends + green_sends + diag_sends + near_sends + far_sends:
        c.wait_send()


def on_device(slices, sites, field, momenta, start_force, green, forward_prop, back_prop, accept):
    size = field.shape[1]
    rows = green.shape[1]
    group = group_of(slices)
    groups = slices // group
    chunks = 4
    row = jax.ShapeDtypeStruct(field.shape, F32)
    bf = jnp.bfloat16
    dma = pltpu.SemaphoreType.DMA
    any_space = pl.BlockSpec(memory_space=pl.ANY)
    vmem = pl.BlockSpec(memory_space=pltpu.VMEM)
    smem = pl.BlockSpec(memory_space=pltpu.SMEM)
    return pl.pallas_call(
        functools.partial(kernel, slices, sites, group, slices * field.shape[0] * size),
        out_shape=(row, row, row, jax.ShapeDtypeStruct((1,), F32)),
        in_specs=[any_space] * 6 + [smem],
        out_specs=(vmem, vmem, vmem, smem),
        scratch_shapes=[
            pltpu.VMEM((3, 1, size), F32),
            pltpu.VMEM((3, 1, size), F32),
            pltpu.VMEM((rows, size), bf),
            pltpu.VMEM((rows, size), bf),
            pltpu.VMEM((2, rows, rows), bf),
            pltpu.VMEM((rows, size), bf),
            pltpu.VMEM((2, rows, LANES), F32),
            pltpu.VMEM((1, size), F32),
            pltpu.VMEM((rows, size), F32),
            pltpu.VMEM((rows, LANES), F32),
            pltpu.VMEM((1, rows), F32),
            pltpu.VMEM((sites, 1, rows), F32),
            pltpu.VMEM((group * sites, 1, LANES), F32),
            pltpu.VMEM((groups, 1, LANES), F32),
            dma((3,)), dma((chunks + 3,)),
            dma((3,)), dma((3,)),
            dma((chunks,)), dma((chunks,)),
            dma((sites,)), dma((sites,)),
            dma((group * sites,)), dma((group * sites,)),
            dma((groups,)), dma((groups,)),
        ],
        compiler_params=pltpu.CompilerParams(
            collective_id=0, has_side_effects=True, vmem_limit_bytes=60 * 1024 * 1024
        ),
        name="leapfrog",
    )(field, momenta, start_force, green, forward_prop, back_prop, accept)


def solution(mesh):
    return jax.shard_map(
        functools.partial(on_device, mesh.shape["cuts"], mesh.shape["site"]),
        mesh=mesh,
        in_specs=(
            P("cuts", None),
            P("cuts", None),
            P("cuts", None),
            P("cuts", "site", None),
            P("site", None),
            P("site", None),
            P("cuts"),
        ),
        out_specs=(P("cuts", None), P("cuts", None), P("cuts", None), P()),
        check_vma=False,
    )
```

time: 118 us -> 39.3 us (0.33)
  blocking collectives: 40.8 us -> 0 us
  Pallas kernels: 0 us -> 32 us
  waiting for transfers between devices: 20.1 us -> 0 us
  between operations: 19.7 us -> 3.03 us
  matrix products: 14.1 us -> 0 us
  starting transfers between devices: 8.79 us -> 0 us
  other arithmetic: 7.51 us -> 0 us
  local copies, waits for them, and re-layouts: 6.42 us -> 3.89 us
    psum x1 -> x0, blocking collectives: 39 us -> none  [on_device(): total = lax.psum(end_local, 'cuts') - start_total]
    pallas_call x0 -> x1, Pallas kernels: none -> 32 us  [on_device(): pl.pallas_call(functools.partial(kernel, slices, sites, group, slices * f...]
    all_gather x1 -> x0, waiting for transfers between devices: 15.2 us -> none  [on_device(): lax.all_gather(scaled, 'site', axis=0, tiled=True)]
    dot_general x1 -> x0, matrix products: 14.1 us -> none  [on_device(): jnp.dot(forward_prop, lax.all_gather(scaled, 'site', axis=0, tiled=True),...]
    ppermute x2 -> x0, starting transfers between devices: 8.75 us -> none  [from_behind(): lax.ppermute(shard, axis, [(i, (i + by) % size) for i in range(size)])]
    convert_element_type x1 -> x0, other arithmetic: 4.89 us -> none  [on_device(): (row_growth[:, None] * source.astype(jnp.float32)).astype(jnp.bfloat16)]
    ppermute x2 -> x0, waiting for transfers between devices: 4.89 us -> none  [from_behind(): lax.ppermute(shard, axis, [(i, (i + by) % size) for i in range(size)])]
    reduce_sum x2 -> x0, other arithmetic: 2.6 us -> none  [on_device(): end_local = jnp.sum(new_momenta * new_momenta) + jnp.sum(trial * trial)]
  transfers between devices with their start and end apart: 3 -> 0, of which waited for: 3 -> 0; matrix products, arithmetic and copies ran while one was open for 5% -> 0% of each run, Pallas kernels for 0% -> 0%
where the time goes in v1:
time: 39.3 us; the launch traced here: 38.9 us
  Pallas kernels  32 us (81%)
  local copies, waits for them, and re-layouts  3.89 us (10%)
  between operations  3.03 us (8%)
    pallas_call x1, Pallas kernels, on_device(): pl.pallas_call(functools.partial(kernel, slices, sites, group, slices * f...  32 us
    unnamed x3, local copies, waits for them, and re-layouts  3.89 us

profile of v1, /device:TPU:0, one launch (start us, length us, event | category | flops | bytes accessed | tf_op | source)
XLA Modules:
  0.0 38.9 jit_solution(16935993916933785852)
XLA Ops:
  1.3 32.0 %leapfrog.1 = (f32[1,2048]{1,0:T(1,128)}, f32[1,2048]{1,0:T(1,128)}, f32[1,2048]{1,0:T(1,128)}, f32[1]{0:T(128)}) custom-call(f32[1,2048]{1,0:T(1,128)} %field.1, f32[1,2048]{1,0:T(1,128)} %momenta.1, f32[1,2048]{1,0:T(1,128)} %force.1, bf16[1,1024,2048]{2,1,0:T(8,128)(2,1)} %green.1, bf16[1024,2048]{1,0:T(8,128)(2,1)} %forward.1, bf16[1024,2048]{1,0:T(8,128)(2,1)} %back.1, ...), custom_call_target="tpu_custom_call" | custom-call | tf_op jit(solution)/shard_map/leapfrog/pallas_call | solution.py:250
  33.2 1.3 %copy.16 = f32[1,2048]{1,0:T(1,128)} copy(f32[1,2048]{1,0:T(1,128)} %get-tuple-element.8) | data formatting | bytes 16384
  34.5 1.3 %copy.17 = f32[1,2048]{1,0:T(1,128)} copy(f32[1,2048]{1,0:T(1,128)} %get-tuple-element.9) | data formatting | bytes 16384
  35.8 1.3 %copy.18 = f32[1,2048]{1,0:T(1,128)} copy(f32[1,2048]{1,0:T(1,128)} %get-tuple-element.10) | data formatting | bytes 16384

commit v2 on v1

--- a/solution.py
+++ b/solution.py
@@ -15,8 +15,8 @@
 MESH = pl.DeviceIdType.MESH
 
 
-def group_of(slices):
-    return max(d for d in range(1, slices + 1) if slices % d == 0 and d * d <= slices)
+def group_of(slices, sites):
+    return max(d for d in range(1, slices + 1) if slices % d == 0 and d * sites <= 32)
 
 
 def half_of(momenta, force):
@@ -24,9 +24,9 @@
 
 
 def kernel(
-    slices, sites, group, count,
-    field, momenta, force, green, forward, back, accept,
-    new_field, new_momenta, new_force, change,
+    slices, sites, group,
+    field, momenta, force, green, forward, back,
+    packed,
     own, ahead, mine, other, fwd, bck, grow, shrink, acc, part, diag_out, diag_in, near, far,
     row_sem, load_sem, row_send, row_recv, green_send, green_recv,
     diag_send, diag_recv, near_send, near_recv, far_send, far_recv,
@@ -115,7 +115,7 @@
 
     half = half_of(own[1], own[2])
     trial = own[0] + stepsize * half
-    new_field[...] = jnp.where(accept[0] == 1, trial, own[0])
+    packed[:, :size] = trial
 
     for c in row_sends:
         c.wait_recv()
@@ -221,24 +221,33 @@
         pltpu.make_async_copy(diag_in.at[s], diag_in.at[s], diag_recv.at[s]).wait()
     diagonal = jnp.concatenate([diag_in[s] for s in range(sites)], axis=1)
     force_now = trial - 2.0 * coupling * (1.0 - 2.0 * diagonal)
-    new_force[...] = force_now
-    new_momenta[...] = half - 0.5 * stepsize * force_now
+    packed[:, size:2 * size] = half - 0.5 * stepsize * force_now
+    packed[:, 2 * size:3 * size] = force_now
 
     for peer, _ in far_peers:
         pltpu.make_async_copy(far.at[peer], far.at[peer], far_recv.at[peer]).wait()
     lump = far[0]
     for i in range(1, groups):
         lump = lump + far[i]
-    change[0] = jnp.sum(lump) * (1.0 / (2.0 * count ** 0.5))
+    packed[:, 3 * size:] = lump
 
     for c in row_sends + green_sends + diag_sends + near_sends + far_sends:
         c.wait_send()
+
+
+def split(count, packed, field, accept, new_field, new_momenta, new_force, change):
+    size = new_field.shape[1]
+    taken = accept[0]
+    new_field[...] = jnp.where(taken == 1, packed[:, :size], field[...])
+    new_momenta[...] = packed[:, size:2 * size]
+    new_force[...] = packed[:, 2 * size:3 * size]
+    change[0] = jnp.sum(packed[:, 3 * size:]) * (1.0 / (2.0 * count ** 0.5))
 
 
 def on_device(slices, sites, field, momenta, start_force, green, forward_prop, back_prop, accept):
     size = field.shape[1]
     rows = green.shape[1]
-    group = group_of(slices)
+    group = group_of(slices, sites)
     groups = slices // group
     chunks = 4
     row = jax.ShapeDtypeStruct(field.shape, F32)
@@ -247,11 +256,11 @@
     any_space = pl.BlockSpec(memory_space=pl.ANY)
     vmem = pl.BlockSpec(memory_space=pltpu.VMEM)
     smem = pl.BlockSpec(memory_space=pltpu.SMEM)
-    return pl.pallas_call(
-        functools.partial(kernel, slices, sites, group, slices * field.shape[0] * size),
-        out_shape=(row, row, row, jax.ShapeDtypeStruct((1,), F32)),
-        in_specs=[any_space] * 6 + [smem],
-        out_specs=(vmem, vmem, vmem, smem),
+    packed = pl.pallas_call(
+        functools.partial(kernel, slices, sites, group),
+        out_shape=jax.ShapeDtypeStruct((1, 3 * size + LANES), F32),
+        in_specs=[any_space] * 6,
+        out_specs=vmem,
         scratch_shapes=[
             pltpu.VMEM((3, 1, size), F32),
             pltpu.VMEM((3, 1, size), F32),
@@ -278,7 +287,14 @@
             collective_id=0, has_side_effects=True, vmem_limit_bytes=60 * 1024 * 1024
         ),
         name="leapfrog",
-    )(field, momenta, start_force, green, forward_prop, back_prop, accept)
+    )(field, momenta, start_force, green, forward_prop, back_prop)
+    return pl.pallas_call(
+        functools.partial(split, slices * field.shape[0] * size),
+        out_shape=(row, row, row, jax.ShapeDtypeStruct((1,), F32)),
+        in_specs=[vmem, vmem, smem],
+        out_specs=(vmem, vmem, vmem, smem),
+        name="split",
+    )(packed, field, accept)
 
 
 def solution(mesh):

time: 39.3 us -> 33.5 us (0.85)
  local copies, waits for them, and re-layouts: 3.89 us -> 0 us
  between operations: 3.03 us -> 1.29 us
    unnamed x3 -> x0, local copies, waits for them, and re-layouts: 3.89 us -> none
    pallas_call x1 -> x2, Pallas kernels: 32 us -> 32 us  [the longest x1 30.7 us: on_device(): pl.pallas_call(functools.partial(kernel, slices, sites, group), out_shape...]
where the time goes in v2:
time: 33.5 us; the launch traced here: 33.3 us
  Pallas kernels  32 us (96%)
  between operations  1.29 us (4%)
    pallas_call x1, Pallas kernels, on_device(): pl.pallas_call(functools.partial(kernel, slices, sites, group), out_shape...  30.7 us
    pallas_call x1, Pallas kernels, on_device(): pl.pallas_call(functools.partial(split, slices * field.shape[0] * size),...  1.38 us

profile of v2, /device:TPU:0, one launch (start us, length us, event | category | flops | bytes accessed | tf_op | source)
XLA Modules:
  0.0 33.3 jit_solution(7099097630765069262)
XLA Ops:
  1.3 30.7 %leapfrog.1.packed = f32[1,6272]{1,0:T(1,128)} custom-call(f32[1,2048]{1,0:T(1,128)} %field.3, f32[1,2048]{1,0:T(1,128)} %momenta.1, f32[1,2048]{1,0:T(1,128)} %force.1, bf16[1,1024,2048]{2,1,0:T(8,128)(2,1)} %green.1, bf16[1024,2048]{1,0:T(8,128)(2,1)} %forward.1, bf16[1024,2048]{1,0:T(8,128)(2,1)} %back.1), custom_call_target="tpu_custom_call" | custom-call | tf_op jit(solution)/shard_map/leapfrog/pallas_call | solution.py:259
  31.9 1.4 %split.1 = (f32[1,2048]{1,0:T(1,128)}, f32[1,2048]{1,0:T(1,128)}, f32[1,2048]{1,0:T(1,128)}, f32[1]{0:T(128)}) custom-call(f32[1,6272]{1,0:T(1,128)} %leapfrog.1.packed, f32[1,2048]{1,0:T(1,128)} %field.3, s32[1]{0:T(128)S(6)} %copy.11.accept), custom_call_target="tpu_custom_call" | custom-call | tf_op jit(solution)/shard_map/split/pallas_call | solution.py:291

commit v3 on v2

--- a/solution.py
+++ b/solution.py
@@ -94,13 +94,17 @@
 
     row_sends = [
         pltpu.make_async_remote_copy(
-            own.at[i], ahead.at[i], row_send.at[i], row_recv.at[i],
-            device_id={"cuts": behind, "site": site}, device_id_type=MESH,
-        )
-        for i in range(3)
-    ]
-    for c in row_sends:
-        c.start()
+            own.at[i], ahead.at[i], row_send.at[3 * s + i], row_recv.at[i],
+            device_id={"cuts": behind, "site": s}, device_id_type=MESH,
+        )
+        for s in range(sites) for i in range(3)
+    ]
+
+    @pl.when(site == sites - 1)
+    def _():
+        for c in row_sends:
+            c.start()
+
     green_sends = [
         pltpu.make_async_remote_copy(
             mine.at[pl.ds(i * deep, deep)], other.at[pl.ds(i * deep, deep)],
@@ -117,8 +121,8 @@
     trial = own[0] + stepsize * half
     packed[:, :size] = trial
 
-    for c in row_sends:
-        c.wait_recv()
+    for i in range(3):
+        pltpu.make_async_copy(ahead.at[i], ahead.at[i], row_recv.at[i]).wait()
     phase = ahead[0] + stepsize * half_of(ahead[1], ahead[2])
     shrink[...] = jnp.exp(-coupling * phase)
     ahead_rows = pl.ds(pl.multiple_of(site * rows, LANES), rows)
@@ -231,7 +235,12 @@
         lump = lump + far[i]
     packed[:, 3 * size:] = lump
 
-    for c in row_sends + green_sends + diag_sends + near_sends + far_sends:
+    @pl.when(site == sites - 1)
+    def _():
+        for c in row_sends:
+            c.wait_send()
+
+    for c in green_sends + diag_sends + near_sends + far_sends:
         c.wait_send()
 
 
@@ -277,7 +286,7 @@
             pltpu.VMEM((group * sites, 1, LANES), F32),
             pltpu.VMEM((groups, 1, LANES), F32),
             dma((3,)), dma((chunks + 3,)),
-            dma((3,)), dma((3,)),
+            dma((3 * sites,)), dma((3,)),
             dma((chunks,)), dma((chunks,)),
             dma((sites,)), dma((sites,)),
             dma((group * sites,)), dma((group * sites,)),

time: 33.5 us -> 33 us (0.985)
  Pallas kernels: 32 us -> 31.5 us
    pallas_call x1, Pallas kernels: 30.7 us -> 30.1 us  [on_device(): pl.pallas_call(functools.partial(kernel, slices, sites, group), out_shape...]
where the time goes in v3:
time: 33 us; the launch traced here: 32.8 us
  Pallas kernels  31.5 us (95%)
  between operations  1.29 us (4%)
    pallas_call x1, Pallas kernels, on_device(): pl.pallas_call(functools.partial(kernel, slices, sites, group), out_shape...  30.1 us
    pallas_call x1, Pallas kernels, on_device(): pl.pallas_call(functools.partial(split, slices * field.shape[0] * size),...  1.38 us

profile of v3, /device:TPU:0, one launch (start us, length us, event | category | flops | bytes accessed | tf_op | source)
XLA Modules:
  0.0 32.8 jit_solution(15432648448183102618)
XLA Ops:
  1.3 30.1 %leapfrog.1.packed = f32[1,6272]{1,0:T(1,128)} custom-call(f32[1,2048]{1,0:T(1,128)} %field.3, f32[1,2048]{1,0:T(1,128)} %momenta.1, f32[1,2048]{1,0:T(1,128)} %force.1, bf16[1,1024,2048]{2,1,0:T(8,128)(2,1)} %green.1, bf16[1024,2048]{1,0:T(8,128)(2,1)} %forward.1, bf16[1024,2048]{1,0:T(8,128)(2,1)} %back.1), custom_call_target="tpu_custom_call" | custom-call | tf_op jit(solution)/shard_map/leapfrog/pallas_call | solution.py:268
  31.4 1.4 %split.1 = (f32[1,2048]{1,0:T(1,128)}, f32[1,2048]{1,0:T(1,128)}, f32[1,2048]{1,0:T(1,128)}, f32[1]{0:T(128)}) custom-call(f32[1,6272]{1,0:T(1,128)} %leapfrog.1.packed, f32[1,2048]{1,0:T(1,128)} %field.3, s32[1]{0:T(128)S(6)} %copy.11.accept), custom_call_target="tpu_custom_call" | custom-call | tf_op jit(solution)/shard_map/split/pallas_call | solution.py:300
